TPU v7x, 32 devices: a whole 2x2x4 slice. The times are simulated.
32 devices in a mesh: rep: 2 (over core), seq: 16 (over z, y, x).
Axes of the slice: x: 2, y: 2, z: 4, core: 2. Of those that a mesh axis runs over, the one named last changes fastest.
Arguments:
- queries: bfloat16 [4096, 8192], P(('rep', 'seq')), parts along dimension 0, may hold values from -180 to 180
- keys: bfloat16 [16384, 1024], P(('rep', 'seq')), parts along dimension 0, may hold values from -6 to 6
- values: bfloat16 [16384, 1024], P(('rep', 'seq')), parts along dimension 0, may hold values from -6 to 6
- vertical: int32 [128, 64], P('rep'), parts along dimension 0, may hold values from 0 to 127, all different within a row
- vert_count: int32 [128], P('rep'), parts along dimension 0, may hold values from 1 to 64
- slash: int32 [128, 32], P('rep'), parts along dimension 0, may hold values from 0 to 95, all different within a row
- slash_count: int32 [128], P('rep'), parts along dimension 0, may hold values from 1 to 32
Outputs:
- attended: bfloat16 [4096, 8192], P(('rep', 'seq')), parts along dimension 0
There are 2 independent parts, one for each index of `rep`. A program takes and returns all parts, laid end to end along the dimension named above; each array names one. Nothing has to cross between parts.
Inputs may be any that keep to these rules, and one draw needn't show every extreme that they name: `vertical`: each row holds 64 different key block numbers; head h uses the first vert_count[h] of them. `slash`: each row holds 32 different numbers; head h uses the first slash_count[h] of them, each number s naming the slash offset s + 1 blocks.
All inputs are finite; a program needn't handle non-finite values.
Results may differ from a plain program's by a relative error of at most 0.007.
Values may be sent and summed in bfloat16 or wider, within the bound.
No kernel may reach another device: no remote copies, remote signals or barrier semaphores. Data moves between devices by JAX's collectives and lax.ppermute only.
A program may use at most 128 MiB of HBM per device.

v0:
```python
import math
import jax
import jax.numpy as jnp
from jax import lax
from jax.sharding import PartitionSpec as P

QUERY_HEADS = 64
KV_HEADS = 8
HEAD_DIM = 128
BLOCK = 64
TURN = 4


def swapped(x, axis, bit):
    return lax.ppermute(x, axis, [(i, i ^ 1 << bit) for i in range(lax.axis_size(axis))])


def absorb(state, scores, valid, combine):
    peak, total, summed = state
    scores = jnp.where(valid, scores, -jnp.inf)
    new_peak = jnp.maximum(peak, jnp.max(scores, axis=1))
    factor = jnp.exp(peak - new_peak)
    weights = jnp.exp(scores - new_peak[:, None])
    total = total * factor + jnp.sum(weights, axis=1)
    summed = summed * factor[:, None] + combine(weights.astype(jnp.bfloat16))
    return (new_peak, total, summed)


def attend(
    query_blocks, storage, slot_of, head, first, stride, vertical, vert_count, slash, slash_count
):
    count_rows, block, width = query_blocks.shape
    total_blocks = storage.shape[0] // block
    cache = storage.reshape(total_blocks, block, 2 * width)
    scale = 1.0 / math.sqrt(width)
    rows = count_rows * block
    absolute = (
        total_blocks
        - count_rows * stride
        + first
        + stride * jnp.arange(count_rows, dtype=jnp.int32)
    )
    verticals = vertical[head]
    live_vert = vert_count[head]
    offsets = slash[head] + 1
    live_slash = slash_count[head]
    lanes = jnp.arange(TURN, dtype=jnp.int32)
    marks = jnp.arange(verticals.shape[0], dtype=jnp.int32) < live_vert
    flat_query = query_blocks.reshape(rows, width)
    diagonal = cache[slot_of(absolute)]
    scores = (
        jnp.einsum(
            "rqd,rkd->rqk", query_blocks, diagonal[:, :, :width], preferred_element_type=jnp.float32
        )
        * scale
    )
    causal = jnp.arange(block)[:, None] >= jnp.arange(block)[None, :]
    scores = jnp.where(causal[None], scores, -jnp.inf)
    peak = jnp.max(scores, axis=2)
    weights = jnp.exp(scores - peak[:, :, None])
    total = jnp.sum(weights, axis=2)
    summed = jnp.einsum(
        "rqk,rkd->rqd",
        weights.astype(jnp.bfloat16),
        diagonal[:, :, width:],
        preferred_element_type=jnp.float32,
    )
    state = (peak.reshape(rows), total.reshape(rows), summed.reshape(rows, width))

    def widen(usable):
        return jnp.broadcast_to(usable[:, None, :, None], (count_rows, block, TURN, block)).reshape(
            rows, TURN * block
        )

    def vertical_turn(step, state):
        picked = lax.dynamic_slice_in_dim(verticals, step * TURN, TURN)
        keys_here = cache[slot_of(picked)].reshape(TURN * block, 2 * width)
        scores = (
            lax.dot_general(
                flat_query,
                keys_here[:, :width],
                (((1,), (1,)), ((), ())),
                preferred_element_type=jnp.float32,
            )
            * scale
        )
        usable = (step * TURN + lanes < live_vert)[None, :] & (picked[None, :] < absolute[:, None])

        def combine(rounded):
            return jnp.dot(rounded, keys_here[:, width:], preferred_element_type=jnp.float32)

        return absorb(state, scores, widen(usable), combine)

    state = lax.fori_loop(0, (live_vert + TURN - 1) // TURN, vertical_turn, state)

    def slash_turn(step, state):
        picked = lax.dynamic_slice_in_dim(offsets, step * TURN, TURN)
        target = absolute[:, None] - picked[None, :]
        keys_here = cache[slot_of(target)].reshape(count_rows, TURN * block, 2 * width)
        scores = (
            jnp.einsum(
                "rqd,rkd->rqk",
                query_blocks,
                keys_here[:, :, :width],
                preferred_element_type=jnp.float32,
            ).reshape(rows, TURN * block)
            * scale
        )
        covered = jnp.any(
            (target[:, :, None] == verticals[None, None, :]) & marks[None, None, :], axis=2
        )
        usable = (step * TURN + lanes < live_slash)[None, :] & jnp.logical_not(covered)

        def combine(rounded):
            return jnp.einsum(
                "rqk,rkd->rqd",
                rounded.reshape(count_rows, block, TURN * block),
                keys_here[:, :, width:],
                preferred_element_type=jnp.float32,
            ).reshape(rows, width)

        return absorb(state, scores, widen(usable), combine)

    state = lax.fori_loop(0, (live_slash + TURN - 1) // TURN, slash_turn, state)
    peak, total, summed = state
    return (summed / total[:, None]).astype(jnp.bfloat16).reshape(count_rows, block, width)


def body(queries, keys, values, vertical, vert_count, slash, slash_count):
    seq_count = lax.axis_size("seq")
    position = lax.axis_index("seq")
    query_rows = queries.shape[0]
    key_rows = keys.shape[0]
    group_devices = seq_count // KV_HEADS
    local_cache = jnp.concatenate(
        [keys.reshape(key_rows, KV_HEADS, HEAD_DIM), values.reshape(key_rows, KV_HEADS, HEAD_DIM)],
        axis=2,
    )
    piece_rows = key_rows // group_devices
    pieces = (
        local_cache.reshape(group_devices, piece_rows, KV_HEADS, 2 * HEAD_DIM)
        .transpose(1, 2, 0, 3)
        .reshape(piece_rows, seq_count, 2 * HEAD_DIM)
    )
    stacked = lax.all_to_all(pieces, "seq", split_axis=1, concat_axis=0, tiled=True).reshape(
        1, seq_count * piece_rows, 2 * HEAD_DIM
    )
    for level in range(group_devices.bit_length() - 1):
        partner = swapped(stacked, "seq", level)
        upper_side = position // 2**level % 2 == 1
        lower = jnp.where(upper_side, partner, stacked)
        upper = jnp.where(upper_side, stacked, partner)
        stacked = jnp.concatenate([lower, upper], axis=0)
    storage = stacked.reshape(group_devices * seq_count * piece_rows, 2 * HEAD_DIM)
    device_blocks = key_rows // BLOCK
    piece_blocks = piece_rows // BLOCK

    def slot_of(index):
        sender = index // device_blocks
        within = index % device_blocks
        return (
            within // piece_blocks * (seq_count * piece_blocks)
            + sender * piece_blocks
            + within % piece_blocks
        )

    per_device = QUERY_HEADS // seq_count
    blocks = queries.reshape(query_rows // BLOCK, BLOCK, QUERY_HEADS, HEAD_DIM)
    gathered = lax.all_to_all(blocks, "seq", split_axis=2, concat_axis=0, tiled=True)
    results = []
    for local in range(per_device):
        results.append(
            attend(
                gathered[:, :, local, :],
                storage,
                slot_of,
                position * per_device + local,
                0,
                1,
                vertical,
                vert_count,
                slash,
                slash_count,
            )
        )
    answer = lax.all_to_all(
        jnp.stack(results, axis=2), "seq", split_axis=0, concat_axis=2, tiled=True
    )
    return answer.reshape(query_rows, QUERY_HEADS * HEAD_DIM)


def solution(mesh):
    return jax.shard_map(
        body,
        mesh=mesh,
        in_specs=(
            P(("rep", "seq"), None),
            P(("rep", "seq"), None),
            P(("rep", "seq"), None),
            P("rep", None),
            P("rep"),
            P("rep", None),
            P("rep"),
        ),
        out_specs=P(("rep", "seq"), None),
        check_vma=False,
    )
```

profile of v0, /device:TPU:0, one launch (start us, length us, event | category | flops | bytes accessed | tf_op | source)
XLA Modules:
  0.0 1188.1 jit_solution(315355499021703888)
XLA Ops:
  3.9 8.3 all-to-all-start
  17.1 38.2 %all-to-all-done = bf16[256,16,256]{2,0,1:T(8,128)(2,1)S(1)} async-done(((bf16[256,16,256]{2,0,1:T(8,128)(2,1)}), bf16[256,16,256]{2,0,1:T(8,128)(2,1)S(1)}, u32[]{:S(2)}, u32[]{:S(2)}) %all-to-all-start) | async-done | bytes 2097184 | tf_op jit(solution)/shard_map/all_to_all | solution.py:145
  56.6 10.0 all-to-all-start.1
  76.7 32.6 %all-to-all-done.1 = bf16[2,64,64,128]{3,1,0,2:T(8,128)(2,1)S(1)} async-done(((bf16[2,64,64,128]{3,1,0,2:T(8,128)(2,1)}), bf16[2,64,64,128]{3,1,0,2:T(8,128)(2,1)S(1)}, u32[]{:S(2)}, u32[]{:S(2)}) %all-to-all-start.1) | async-done | bytes 2097184 | tf_op jit(solution)/shard_map/all_to_all | solution.py:169
  112.2 23.4 %collective-permute-done = bf16[1,4096,256]{2,1,0:T(8,128)(2,1)} collective-permute-done((bf16[1,4096,256]{2,1,0:T(8,128)(2,1)}, bf16[1,4096,256]{2,1,0:T(8,128)(2,1)}, u32[]{:S(2)}, u32[]{:S(2)}) %collective-permute-start) | collective-permute-done | bytes 2097184 | tf_op jit(solution)/shard_map/ppermute | solution.py:15
  155.0 12.7 %while.148 = (s32[]{:T(128)}, f32[2048]{0:T(1024)S(1)}, f32[2048]{0:T(1024)S(1)}, f32[2048,128]{1,0:T(8,128)S(1)}, s32[]{:T(128)}, /*index=5*/s32[]{:T(128)}, s3...) while((s32[]{:T(128)}, f32[2048]{0:T(1024)S(1)}, ...), condition=%wide.region_5.6_spmd.clone, body=%wide.region_2.5_spmd.clone.sunk | while | flops 272635360 | bytes 11539231 | solution.py:94
  167.7 126.9 %while.152 = (s32[]{:T(128)}, f32[2048]{0:T(1024)S(1)}, f32[2048]{0:T(1024)S(1)}, f32[2048,128]{1,0:T(8,128)S(1)}, s32[]{:T(128)}, /*index=5*/s32[]{:T(128)}, s3...) while((s32[]{:T(128)}, f32[2048]{0:T(1024)S(1)}, ...), condition=%wide.region_10.11_spmd.clone.clone, body=%wide.region_6.10_spmd.clone.clone.sunk | while | flops 274762880 | bytes 32220464 | solution.py:124
  170.1 5.0 gather_fusion
  188.2 5.0 gather_fusion
  206.3 5.0 gather_fusion
  224.5 5.0 gather_fusion
  242.6 5.0 gather_fusion
  260.7 5.0 gather_fusion
  295.7 195.0 %while.149 = (s32[]{:T(128)}, f32[2048]{0:T(1024)S(1)}, f32[2048]{0:T(1024)S(1)}, f32[2048,128]{1,0:T(8,128)S(1)}, s32[]{:T(128)}, /*index=5*/s32[]{:T(128)}, s3...) while((s32[]{:T(128)}, f32[2048]{0:T(1024)S(1)}, ...), condition=%wide.region_16.17_spmd.clone, body=%wide.region_13.16_spmd.clone.sunk | while | flops 272635360 | bytes 11539231 | solution.py:94
  490.7 125.9 %while.153 = (s32[]{:T(128)}, f32[2048]{0:T(1024)S(1)}, f32[2048]{0:T(1024)S(1)}, f32[2048,128]{1,0:T(8,128)S(1)}, s32[]{:T(128)}, /*index=5*/s32[]{:T(128)}, s3...) while((s32[]{:T(128)}, f32[2048]{0:T(1024)S(1)}, ...), condition=%wide.region_21.22_spmd.clone.clone, body=%wide.region_17.21_spmd.clone.clone.sunk | while | flops 274762880 | bytes 34317640 | solution.py:124
  493.1 5.0 gather_fusion.1
  508.8 5.0 gather_fusion.1
  524.6 5.0 gather_fusion.1
  540.3 5.0 gather_fusion.1
  556.0 5.0 gather_fusion.1
  571.7 5.0 gather_fusion.1
  587.4 5.0 gather_fusion.1
  603.1 5.0 gather_fusion.1
  616.7 81.9 %while.150 = (s32[]{:T(128)}, f32[2048]{0:T(1024)S(1)}, f32[2048]{0:T(1024)S(1)}, f32[2048,128]{1,0:T(8,128)S(1)}, s32[]{:T(128)}, /*index=5*/s32[]{:T(128)}, s3...) while((s32[]{:T(128)}, f32[2048]{0:T(1024)S(1)}, ...), condition=%wide.region_27.28_spmd.clone, body=%wide.region_24.27_spmd.clone.sunk | while | flops 272635360 | bytes 11539231 | solution.py:94
  698.7 126.0 %while.154 = (s32[]{:T(128)}, f32[2048]{0:T(1024)S(1)}, f32[2048]{0:T(1024)S(1)}, f32[2048,128]{1,0:T(8,128)S(1)}, s32[]{:T(128)}, /*index=5*/s32[]{:T(128)}, s3...) while((s32[]{:T(128)}, f32[2048]{0:T(1024)S(1)}, ...), condition=%wide.region_32.33_spmd.clone.clone, body=%wide.region_28.32_spmd.clone.clone.sunk | while | flops 274762880 | bytes 32220464 | solution.py:124
  737.1 5.0 gather_fusion.2
  773.0 5.0 gather_fusion.2
  809.0 5.0 gather_fusion.2
  824.8 61.2 %while.151 = (s32[]{:T(128)}, f32[2048]{0:T(1024)S(1)}, f32[2048]{0:T(1024)S(1)}, f32[2048,128]{1,0:T(8,128)S(1)}, s32[]{:T(128)}, /*index=5*/s32[]{:T(128)}, s3...) while((s32[]{:T(128)}, f32[2048]{0:T(1024)S(1)}, ...), condition=%wide.region_38.39_spmd.clone, body=%wide.region_35.38_spmd.clone.sunk | while | flops 272635360 | bytes 11539231 | solution.py:94
  886.0 35.8 %while.155 = (s32[]{:T(128)}, f32[2048]{0:T(1024)S(1)}, f32[2048]{0:T(1024)S(1)}, f32[2048,128]{1,0:T(8,128)S(1)}, s32[]{:T(128)}, /*index=5*/s32[]{:T(128)}, s3...) while((s32[]{:T(128)}, f32[2048]{0:T(1024)S(1)}, ...), condition=%wide.region_43.44_spmd.clone.clone, body=%wide.region_39.43_spmd.clone.clone.sunk | while | flops 274762880 | bytes 32220464 | solution.py:124
  888.3 5.0 gather_fusion.3
  924.7 258.7 %all_to_all.48 = bf16[32,64,4,128]{3,1,2,0:T(8,128)(2,1)S(1)} all-to-all(bf16[32,64,4,128]{3,1,2,0:T(8,128)(2,1)S(1)} %pad_maximum_fusion.1), channel_id=1, replica_groups=mesh['rep'=2,'seq'=16] {'seq'}, dimensions={0} | all-to-all | bytes 4194304 | tf_op jit(solution)/shard_map/all_to_all | solution.py:186
  (1121 shorter events, 715.4 us)
Async XLA Ops:
  3.9 51.4 %all-to-all-start = ((bf16[256,16,256]{2,0,1:T(8,128)(2,1)}), bf16[256,16,256]{2,0,1:T(8,128)(2,1)S(1)}, u32[]{:S(2)}, u32[]{:S(2)}) async-start(bf16[256,16,256]{2,0,1:T(8,128)(2,1)} %bitcast.1), calls=%async_computation | async-start | bytes 4194304 | tf_op jit(solution)/shard_map/all_to_all | solution.py:145
  17.1 51.5 %copy-start.19 = (s32[64]{0:T(128)S(1)}, s32[64]{0:T(128)}, u32[]{:S(2)}) copy-start(s32[64]{0:T(128)} %param.29) | copy-start | bytes 772
  17.1 51.5 %copy-start.20 = (s32[64]{0:T(128)S(1)}, s32[64]{0:T(128)}, u32[]{:S(2)}) copy-start(s32[64]{0:T(128)} %param.27) | copy-start | bytes 772
  17.1 57.3 %copy-start.16 = (s32[64,32]{0,1:T(8,128)S(1)}, s32[64,32]{0,1:T(8,128)}, u32[]{:S(2)}) copy-start(s32[64,32]{0,1:T(8,128)} %param.28) | copy-start | bytes 24580
  56.6 52.6 %all-to-all-start.1 = ((bf16[2,64,64,128]{3,1,0,2:T(8,128)(2,1)}), bf16[2,64,64,128]{3,1,0,2:T(8,128)(2,1)S(1)}, u32[]{:S(2)}, u32[]{:S(2)}) async-start(bf16[2,64,64,128]{3,1,0,2:T(8,128)(2,1)} %copy.39), calls=%async_computation.1 | async-start | bytes 4194304 | tf_op jit(solution)/shard_map/all_to_all | solution.py:169
  66.7 69.0 %collective-permute-start = (bf16[1,4096,256]{2,1,0:T(8,128)(2,1)}, bf16[1,4096,256]{2,1,0:T(8,128)(2,1)}, u32[]{:S(2)}, u32[]{:S(2)}) collective-permute-start(bf16[1,4096,256]{2,1,0:T(8,128)(2,1)} %bitcast.307), channel_id=1, source_target_pairs={{0,1},{1,0},{2,3},{3,2},{4,5},{5,4},{6,7},{7,6},{8,9},{9,8},{10,11... | collective-permute-start | bytes 6291464 | tf_op jit(solution)/shard_map/ppermute | solution.py:15
  109.5 26.2 %copy-start.10 = (bf16[256,16,256]{2,0,1:T(8,128)(2,1)S(1)}, bf16[256,16,256]{2,0,1:T(8,128)(2,1)}, u32[]{:S(2)}) copy-start(bf16[256,16,256]{2,0,1:T(8,128)(2,1)} %copy-done.9) | copy-start | bytes 6291460
  142.7 4.6 copy-start.6
  179.1 4.1 copy-start.2
  197.2 4.1 copy-start.2
  215.3 4.1 copy-start.2
  233.4 4.1 copy-start.2
  251.6 4.1 copy-start.2
  269.7 4.1 copy-start.2
  287.8 4.1 copy-start.2
  493.1 5.0 copy-start.15
  508.8 5.0 copy-start.15
  524.6 5.0 copy-start.15
  540.3 5.0 copy-start.15
  556.0 5.0 copy-start.15
  571.7 5.0 copy-start.15
  587.4 5.0 copy-start.15
  603.1 5.0 copy-start.15
  698.6 126.0 %copy-start.17 = (f32[32,64]{1,0:T(8,128)S(1)}, f32[32,64]{1,0:T(8,128)}, u32[]{:S(2)}) copy-start(f32[32,64]{1,0:T(8,128)} %fusion.203) | copy-start | bytes 24580
  698.6 126.1 %copy-start = (f32[32,64,128]{2,1,0:T(8,128)S(1)}, f32[32,64,128]{2,1,0:T(8,128)}, u32[]{:S(2)}) copy-start(f32[32,64,128]{2,1,0:T(8,128)} %fusion.204) | copy-start | bytes 3145732
  698.7 126.1 %copy-start.11 = (f32[2048]{0:T(1024)S(1)}, f32[2048]{0:T(1024)}, u32[]{:S(2)}) copy-start(f32[2048]{0:T(1024)} %reshape.1697) | copy-start | bytes 24580
  698.7 126.1 %copy-start.18 = (s32[1,64]{1,0:T(1,128)S(1)}, s32[1,64]{1,0:T(1,128)}, u32[]{:S(2)}) copy-start(s32[1,64]{1,0:T(1,128)} %get-tuple-element.2841) | copy-start | bytes 772
  710.1 4.0 copy-start.4
  728.0 4.0 copy-start.4
  764.0 4.0 copy-start.4
  824.8 61.2 %copy-start.21 = (s32[32]{0:T(128)S(1)}, s32[32]{0:T(128)}, u32[]{:S(2)}) copy-start(s32[32]{0:T(128)} %get-tuple-element.2840) | copy-start | bytes 388
  886.0 35.8 %copy-start.13 = (f32[2048]{0:T(1024)S(1)}, f32[2048]{0:T(1024)}, u32[]{:S(2)}) copy-start(f32[2048]{0:T(1024)} %copy-done.12) | copy-start | bytes 24580
  (20 other events, 57.5 us)
where the time goes:
time: 1200 us; the launch traced here: 1190 us
  local copies, waits for them, and re-layouts  393 us (33%)
  matrix products  271 us (23%)
  blocking collectives  259 us (22%)
  other arithmetic  139 us (12%)
  waiting for transfers between devices  94.2 us (8%)
  starting transfers between devices  20.3 us (2%)
    all_to_all x1, blocking collectives, body(): lax.all_to_all(jnp.stack(results, axis=2), 'seq', split_axis=0, concat_ax...  259 us
    gather x24, local copies, waits for them, and re-layouts, slash_turn(): cache[slot_of(target)].reshape(count_rows, TURN * block, 2 * width)  120 us
    reshape x30, local copies, waits for them, and re-layouts, widen(): jnp.broadcast_to(usable[:, None, :, None], (count_rows, block, TURN, block))  118 us
    dot_general x24, matrix products, slash_turn(): jnp.einsum('rqd,rkd->rqk', query_blocks, keys_here[:, :, :width], preferr...  91.6 us
    dot_general x24, matrix products, combine(): jnp.einsum('rqk,rkd->rqd', rounded.reshape(count_rows, block, TURN * bloc...  88.2 us
    gather x30, local copies, waits for them, and re-layouts, vertical_turn(): keys_here = cache[slot_of(picked)].reshape(TURN * block, 2 * width)  82.2 us
    dot_general x30, matrix products, vertical_turn(): lax.dot_general(flat_query, keys_here[:, :width], (((1,), (1,)), ((), ())...  51.4 us
    all_to_all x1, waiting for transfers between devices, body(): lax.all_to_all(pieces, 'seq', split_axis=1, concat_axis=0, tiled=True)  38.2 us
  transfers between devices with their start and end apart: 3, of which 3 were waited for; matrix products, arithmetic and copies ran while one was open for 1% of the time, Pallas kernels for 0%

commit v1 on v0

--- a/solution.py
+++ b/solution.py
@@ -183,9 +183,19 @@
                 slash_count,
             )
         )
-    answer = lax.all_to_all(
-        jnp.stack(results, axis=2), "seq", split_axis=0, concat_axis=2, tiled=True
-    )
+    shard = jnp.stack(results, axis=2)
+    ways, here = (lax.axis_size("seq"), lax.axis_index("seq"))
+    width_2 = shard.shape[0] // ways
+    shape = list(shard.shape)
+    shape[0] = width_2
+    height = shape[2]
+    shape[2] = height * ways
+    answer = jnp.zeros(shape, shard.dtype)
+    for mask in range(ways):
+        part = lax.dynamic_slice_in_dim(shard, (here ^ mask) * width_2, width_2, axis=0)
+        if mask:
+            part = lax.ppermute(part, "seq", [(d, d ^ mask) for d in range(ways)])
+        answer = lax.dynamic_update_slice_in_dim(answer, part, (here ^ mask) * height, axis=2)
     return answer.reshape(query_rows, QUERY_HEADS * HEAD_DIM)
 
 

time: 1200 us -> 1100 us (0.917)
  blocking collectives: 259 us -> 0 us
  starting transfers between devices: 20.3 us -> 229 us
  local copies, waits for them, and re-layouts: 393 us -> 357 us
  matrix products: 271 us -> 237 us
    all_to_all x1 -> x0, blocking collectives: 259 us -> none  [body(): lax.all_to_all(jnp.stack(results, axis=2), 'seq', split_axis=0, concat_ax...]
    ppermute x0 -> x15, starting transfers between devices: none -> 208 us  [body(): part = lax.ppermute(part, 'seq', [(d, d ^ mask) for d in range(ways)])]
    reshape x30, local copies, waits for them, and re-layouts: 118 us -> 88.7 us  [widen(): jnp.broadcast_to(usable[:, None, :, None], (count_rows, block, TURN, block))]
    broadcast_in_dim x78, local copies, waits for them, and re-layouts: 36.3 us -> 15.9 us  [widen(): jnp.broadcast_to(usable[:, None, :, None], (count_rows, block, TURN, block))]
    dot_general x30, matrix products: 51.4 us -> 35.7 us  [vertical_turn(): lax.dot_general(flat_query, keys_here[:, :width], (((1,), (1,)), ((), ())...]
    ppermute x0 -> x15, waiting for transfers between devices: none -> 15.1 us  [body(): part = lax.ppermute(part, 'seq', [(d, d ^ mask) for d in range(ways)])]
  transfers between devices with their start and end apart: 3 -> 18, of which waited for: 3 -> 9; matrix products, arithmetic and copies ran while one was open for 1% -> 1% of each run, Pallas kernels for 0% -> 0%
where the time goes in v1:
time: 1100 us; the launch traced here: 1080 us
  local copies, waits for them, and re-layouts  357 us (32%)
  matrix products  237 us (22%)
  starting transfers between devices  229 us (21%)
  other arithmetic  140 us (13%)
  waiting for transfers between devices  106 us (10%)
    ppermute x15, starting transfers between devices, body(): part = lax.ppermute(part, 'seq', [(d, d ^ mask) for d in range(ways)])  208 us
    gather x24, local copies, waits for them, and re-layouts, slash_turn(): cache[slot_of(target)].reshape(count_rows, TURN * block, 2 * width)  120 us
    reshape x30, local copies, waits for them, and re-layouts, widen(): jnp.broadcast_to(usable[:, None, :, None], (count_rows, block, TURN, block))  88.7 us
    dot_general x24, matrix products, slash_turn(): jnp.einsum('rqd,rkd->rqk', query_blocks, keys_here[:, :, :width], preferr...  82.7 us
    gather x30, local copies, waits for them, and re-layouts, vertical_turn(): keys_here = cache[slot_of(picked)].reshape(TURN * block, 2 * width)  82.2 us
    dot_general x24, matrix products, combine(): jnp.einsum('rqk,rkd->rqd', rounded.reshape(count_rows, block, TURN * bloc...  80 us
    all_to_all x1, waiting for transfers between devices, body(): lax.all_to_all(pieces, 'seq', split_axis=1, concat_axis=0, tiled=True)  38.2 us
    dot_general x30, matrix products, vertical_turn(): lax.dot_general(flat_query, keys_here[:, :width], (((1,), (1,)), ((), ())...  35.7 us
  transfers between devices with their start and end apart: 18, of which 9 were waited for; matrix products, arithmetic and copies ran while one was open for 1% of the time, Pallas kernels for 0%

profile of v1, /device:TPU:0, one launch (start us, length us, event | category | flops | bytes accessed | tf_op | source)
XLA Modules:
  0.0 1081.3 jit_solution(18215159907768175555)
XLA Ops:
  3.9 8.3 all-to-all-start
  17.1 38.2 %all-to-all-done = bf16[256,16,256]{2,0,1:T(8,128)(2,1)S(1)} async-done(((bf16[256,16,256]{2,0,1:T(8,128)(2,1)}), bf16[256,16,256]{2,0,1:T(8,128)(2,1)S(1)}, u32[]{:S(2)}, u32[]{:S(2)}) %all-to-all-start) | async-done | bytes 2097184 | tf_op jit(solution)/shard_map/all_to_all | solution.py:145
  56.6 10.0 all-to-all-start.1
  76.8 32.4 %all-to-all-done.1 = bf16[2,64,64,128]{3,1,0,2:T(8,128)(2,1)S(1)} async-done(((bf16[2,64,64,128]{3,1,0,2:T(8,128)(2,1)}), bf16[2,64,64,128]{3,1,0,2:T(8,128)(2,1)S(1)}, u32[]{:S(2)}, u32[]{:S(2)}) %all-to-all-start.1) | async-done | bytes 2097184 | tf_op jit(solution)/shard_map/all_to_all | solution.py:169
  115.1 20.6 %collective-permute-done = bf16[1,4096,256]{2,1,0:T(8,128)(2,1)} collective-permute-done((bf16[1,4096,256]{2,1,0:T(8,128)(2,1)}, bf16[1,4096,256]{2,1,0:T(8,128)(2,1)}, u32[]{:S(2)}, u32[]{:S(2)}) %collective-permute-start) | collective-permute-done | bytes 2097184 | tf_op jit(solution)/shard_map/ppermute | solution.py:15
  153.7 12.4 %while.148 = (s32[]{:T(128)}, f32[2048]{0:T(1024)S(1)}, f32[2048]{0:T(1024)S(1)}, f32[2048,128]{1,0:T(8,128)S(1)}, s32[]{:T(128)}, /*index=5*/s32[]{:T(128)}, s3...) while((s32[]{:T(128)}, f32[2048]{0:T(1024)S(1)}, ...), condition=%wide.region_5.6_spmd.clone, body=%wide.region_2.5_spmd.clone.sunk | while | flops 272635360 | bytes 11539231 | solution.py:94
  166.1 126.2 %while.152 = (s32[]{:T(128)}, f32[2048]{0:T(1024)S(1)}, f32[2048]{0:T(1024)S(1)}, f32[2048,128]{1,0:T(8,128)S(1)}, s32[]{:T(128)}, /*index=5*/s32[]{:T(128)}, s3...) while((s32[]{:T(128)}, f32[2048]{0:T(1024)S(1)}, ...), condition=%wide.region_10.11_spmd.clone.clone, body=%wide.region_6.10_spmd.clone.clone.sunk | while | flops 274762880 | bytes 32220464 | solution.py:124
  186.5 5.0 gather_fusion
  222.6 5.0 gather_fusion
  240.6 5.0 gather_fusion
  276.7 5.0 gather_fusion
  294.8 163.6 %while.149 = (s32[]{:T(128)}, f32[2048]{0:T(1024)S(1)}, f32[2048]{0:T(1024)S(1)}, f32[2048,128]{1,0:T(8,128)S(1)}, s32[]{:T(128)}, /*index=5*/s32[]{:T(128)}, s3...) while((s32[]{:T(128)}, f32[2048]{0:T(1024)S(1)}, ...), condition=%wide.region_16.17_spmd.clone, body=%wide.region_13.16_spmd.clone.sunk | while | flops 272635360 | bytes 11539231 | solution.py:94
  458.4 126.1 %while.153 = (s32[]{:T(128)}, f32[2048]{0:T(1024)S(1)}, f32[2048]{0:T(1024)S(1)}, f32[2048,128]{1,0:T(8,128)S(1)}, s32[]{:T(128)}, /*index=5*/s32[]{:T(128)}, s3...) while((s32[]{:T(128)}, f32[2048]{0:T(1024)S(1)}, ...), condition=%wide.region_21.22_spmd.clone.clone, body=%wide.region_17.21_spmd.clone.clone.sunk | while | flops 274762880 | bytes 34317640 | solution.py:124
  461.0 5.0 gather_fusion.1
  476.8 5.0 gather_fusion.1
  492.5 5.0 gather_fusion.1
  508.2 5.0 gather_fusion.1
  523.9 5.0 gather_fusion.1
  539.6 5.0 gather_fusion.1
  555.3 5.0 gather_fusion.1
  571.0 5.0 gather_fusion.1
  587.0 67.3 %while.150 = (s32[]{:T(128)}, f32[2048]{0:T(1024)S(1)}, f32[2048]{0:T(1024)S(1)}, f32[2048,128]{1,0:T(8,128)S(1)}, s32[]{:T(128)}, /*index=5*/s32[]{:T(128)}, s3...) while((s32[]{:T(128)}, f32[2048]{0:T(1024)S(1)}, ...), condition=%wide.region_27.28_spmd.clone, body=%wide.region_24.27_spmd.clone.sunk | while | flops 272635360 | bytes 11539231 | solution.py:94
  654.3 111.4 %while.154 = (s32[]{:T(128)}, f32[2048]{0:T(1024)S(1)}, f32[2048]{0:T(1024)S(1)}, f32[2048,128]{1,0:T(8,128)S(1)}, s32[]{:T(128)}, /*index=5*/s32[]{:T(128)}, s3...) while((s32[]{:T(128)}, f32[2048]{0:T(1024)S(1)}, ...), condition=%wide.region_32.33_spmd.clone.clone, body=%wide.region_28.32_spmd.clone.clone.sunk | while | flops 274762880 | bytes 23831828 | solution.py:124
  656.6 5.0 gather_fusion.2
  768.2 42.2 %while.151 = (s32[]{:T(128)}, f32[2048]{0:T(1024)S(1)}, f32[2048]{0:T(1024)S(1)}, f32[2048,128]{1,0:T(8,128)S(1)}, s32[]{:T(128)}, /*index=5*/s32[]{:T(128)}, s3...) while((s32[]{:T(128)}, f32[2048]{0:T(1024)S(1)}, ...), condition=%wide.region_38.39_spmd.clone, body=%wide.region_35.38_spmd.clone.sunk | while | flops 272635360 | bytes 11539231 | solution.py:94
  810.5 31.4 %while.155 = (s32[]{:T(128)}, f32[2048]{0:T(1024)S(1)}, f32[2048]{0:T(1024)S(1)}, f32[2048,128]{1,0:T(8,128)S(1)}, s32[]{:T(128)}, /*index=5*/s32[]{:T(128)}, s3...) while((s32[]{:T(128)}, f32[2048]{0:T(1024)S(1)}, ...), condition=%wide.region_43.44_spmd.clone.clone, body=%wide.region_39.43_spmd.clone.clone.sunk | while | flops 274762880 | bytes 34317640 | solution.py:124
  812.7 5.0 gather_fusion.3
  828.4 5.0 gather_fusion.3
  851.0 12.2 %collective-permute-start.2 = (bf16[2,64,4,128]{3,2,1,0:T(4,128)(2,1)}, bf16[2,64,4,128]{3,2,1,0:T(4,128)(2,1)}, u32[]{:S(2)}, u32[]{:S(2)}) collective-permute-start(bf16[2,64,4,128]{3,2,1,0:T(4,128)(2,1)} %get-tuple-element.2200), channel_id=1, source_target_pairs={{0,2},{1,3},{2,0},{3,1},{4,6},{5,7},{6,4},{7,5},{8,10},{9,11},{10,... | collective-permute-start | bytes 393224 | tf_op jit(solution)/shard_map/ppermute | solution.py:197
  864.7 170.8 %collective-permute-start.4 = (bf16[2,64,4,128]{3,2,1,0:T(4,128)(2,1)}, bf16[2,64,4,128]{3,2,1,0:T(4,128)(2,1)S(1)}, u32[]{:S(2)}, u32[]{:S(2)}) collective-permute-start(bf16[2,64,4,128]{3,2,1,0:T(4,128)(2,1)} %get-tuple-element.2198), channel_id=1, source_target_pairs={{0,4},{1,5},{2,6},{3,7},{4,0},{5,1},{6,2},{7,3},{8,12},{9,13},{10,... | collective-permute-start | bytes 393224 | tf_op jit(solution)/shard_map/ppermute | solution.py:197
  1052.7 6.9 collective-permute-done.8
  1059.6 5.2 collective-permute-start.13
  (1166 shorter events, 689.4 us)
Async XLA Ops:
  3.9 51.4 %all-to-all-start = ((bf16[256,16,256]{2,0,1:T(8,128)(2,1)}), bf16[256,16,256]{2,0,1:T(8,128)(2,1)S(1)}, u32[]{:S(2)}, u32[]{:S(2)}) async-start(bf16[256,16,256]{2,0,1:T(8,128)(2,1)} %bitcast.1), calls=%async_computation | async-start | bytes 4194304 | tf_op jit(solution)/shard_map/all_to_all | solution.py:145
  17.1 51.5 %copy-start.22 = (s32[64]{0:T(128)S(1)}, s32[64]{0:T(128)}, u32[]{:S(2)}) copy-start(s32[64]{0:T(128)} %param.29) | copy-start | bytes 772
  17.1 51.5 %copy-start.23 = (s32[64]{0:T(128)S(1)}, s32[64]{0:T(128)}, u32[]{:S(2)}) copy-start(s32[64]{0:T(128)} %param.27) | copy-start | bytes 772
  17.1 57.4 %copy-start.19 = (s32[64,32]{0,1:T(8,128)S(1)}, s32[64,32]{0,1:T(8,128)}, u32[]{:S(2)}) copy-start(s32[64,32]{0,1:T(8,128)} %param.28) | copy-start | bytes 24580
  56.6 52.6 %all-to-all-start.1 = ((bf16[2,64,64,128]{3,1,0,2:T(8,128)(2,1)}), bf16[2,64,64,128]{3,1,0,2:T(8,128)(2,1)S(1)}, u32[]{:S(2)}, u32[]{:S(2)}) async-start(bf16[2,64,64,128]{3,1,0,2:T(8,128)(2,1)} %copy.53), calls=%async_computation.1 | async-start | bytes 4194304 | tf_op jit(solution)/shard_map/all_to_all | solution.py:169
  66.7 69.0 %collective-permute-start = (bf16[1,4096,256]{2,1,0:T(8,128)(2,1)}, bf16[1,4096,256]{2,1,0:T(8,128)(2,1)}, u32[]{:S(2)}, u32[]{:S(2)}) collective-permute-start(bf16[1,4096,256]{2,1,0:T(8,128)(2,1)} %bitcast.309), channel_id=1, source_target_pairs={{0,1},{1,0},{2,3},{3,2},{4,5},{5,4},{6,7},{7,6},{8,9},{9,8},{10,11... | collective-permute-start | bytes 6291464 | tf_op jit(solution)/shard_map/ppermute | solution.py:15
  112.4 30.3 %copy-start.8 = (bf16[16,2,64,4,128]{4,2,1,0,3:T(8,128)(2,1)}, bf16[16,2,64,4,128]{4,2,1,0,3:T(8,128)(2,1)S(1)}, u32[]{:S(2)}) copy-start(bf16[16,2,64,4,128]{4,2,1,0,3:T(8,128)(2,1)S(1)} %copy.55) | copy-start | bytes 6291460
  112.4 23.3 %copy-start.11 = (bf16[256,16,256]{2,0,1:T(8,128)(2,1)S(1)}, bf16[256,16,256]{2,0,1:T(8,128)(2,1)}, u32[]{:S(2)}) copy-start(bf16[256,16,256]{2,0,1:T(8,128)(2,1)} %copy-done.10) | copy-start | bytes 6291460
  461.0 5.0 copy-start.18
  476.7 5.0 copy-start.18
  492.5 5.0 copy-start.18
  508.2 5.0 copy-start.18
  523.9 5.0 copy-start.18
  539.6 5.0 copy-start.18
  768.2 42.2 %copy-start.24 = (s32[32]{0:T(128)S(1)}, s32[32]{0:T(128)}, u32[]{:S(2)}) copy-start(s32[32]{0:T(128)} %get-tuple-element.2856) | copy-start | bytes 388
  812.7 5.0 copy-start.17
  828.4 5.0 copy-start.17
  851.0 185.4 %collective-permute-start.1 = (bf16[2,64,4,128]{3,2,1,0:T(4,128)(2,1)}, bf16[2,64,4,128]{3,2,1,0:T(4,128)(2,1)}, u32[]{:S(2)}, u32[]{:S(2)}) collective-permute-start(bf16[2,64,4,128]{3,2,1,0:T(4,128)(2,1)} %get-tuple-element.2201), channel_id=1, source_target_pairs={{0,1},{1,0},{2,3},{3,2},{4,5},{5,4},{6,7},{7,6},{8,9},{9,8},{10,11... | collective-permute-start | bytes 393224 | tf_op jit(solution)/shard_map/ppermute | solution.py:197
  851.0 189.9 %collective-permute-start.2 = (bf16[2,64,4,128]{3,2,1,0:T(4,128)(2,1)}, bf16[2,64,4,128]{3,2,1,0:T(4,128)(2,1)}, u32[]{:S(2)}, u32[]{:S(2)}) collective-permute-start(bf16[2,64,4,128]{3,2,1,0:T(4,128)(2,1)} %get-tuple-element.2200), channel_id=1, source_target_pairs={{0,2},{1,3},{2,0},{3,1},{4,6},{5,7},{6,4},{7,5},{8,10},{9,11},{10,... | collective-permute-start | bytes 393224 | tf_op jit(solution)/shard_map/ppermute | solution.py:197
  863.2 179.4 %collective-permute-start.3 = (bf16[2,64,4,128]{3,2,1,0:T(4,128)(2,1)}, bf16[2,64,4,128]{3,2,1,0:T(4,128)(2,1)S(1)}, u32[]{:S(2)}, u32[]{:S(2)}) collective-permute-start(bf16[2,64,4,128]{3,2,1,0:T(4,128)(2,1)} %get-tuple-element.2199), channel_id=1, source_target_pairs={{0,3},{1,2},{2,1},{3,0},{4,7},{5,6},{6,5},{7,4},{8,11},{9,10},{10,... | collective-permute-start | bytes 393224 | tf_op jit(solution)/shard_map/ppermute | solution.py:197
  864.7 178.2 %collective-permute-start.4 = (bf16[2,64,4,128]{3,2,1,0:T(4,128)(2,1)}, bf16[2,64,4,128]{3,2,1,0:T(4,128)(2,1)S(1)}, u32[]{:S(2)}, u32[]{:S(2)}) collective-permute-start(bf16[2,64,4,128]{3,2,1,0:T(4,128)(2,1)} %get-tuple-element.2198), channel_id=1, source_target_pairs={{0,4},{1,5},{2,6},{3,7},{4,0},{5,1},{6,2},{7,3},{8,12},{9,13},{10,... | collective-permute-start | bytes 393224 | tf_op jit(solution)/shard_map/ppermute | solution.py:197
  1035.5 11.0 %collective-permute-start.5 = (bf16[2,64,4,128]{3,2,1,0:T(4,128)(2,1)S(1)}, bf16[2,64,4,128]{3,2,1,0:T(4,128)(2,1)S(1)}, u32[]{:S(2)}, u32[]{:S(2)}) collective-permute-start(bf16[2,64,4,128]{3,2,1,0:T(4,128)(2,1)S(1)} %get-tuple-element.2197), channel_id=1, source_target_pairs={{0,5},{1,4},{2,7},{3,6},{4,1},{5,0},{6,3},{7,2},{8,13},{9,12},{10,... | collective-permute-start | bytes 393224 | tf_op jit(solution)/shard_map/ppermute | solution.py:197
  1036.4 13.3 %collective-permute-start.6 = (bf16[2,64,4,128]{3,2,1,0:T(4,128)(2,1)S(1)}, bf16[2,64,4,128]{3,2,1,0:T(4,128)(2,1)S(1)}, u32[]{:S(2)}, u32[]{:S(2)}) collective-permute-start(bf16[2,64,4,128]{3,2,1,0:T(4,128)(2,1)S(1)} %get-tuple-element.2196), channel_id=1, source_target_pairs={{0,6},{1,7},{2,4},{3,5},{4,2},{5,3},{6,0},{7,1},{8,14},{9,15},{10,... | collective-permute-start | bytes 393224 | tf_op jit(solution)/shard_map/ppermute | solution.py:197
  1040.9 11.1 %collective-permute-start.7 = (bf16[2,64,4,128]{3,2,1,0:T(4,128)(2,1)S(1)}, bf16[2,64,4,128]{3,2,1,0:T(4,128)(2,1)S(1)}, u32[]{:S(2)}, u32[]{:S(2)}) collective-permute-start(bf16[2,64,4,128]{3,2,1,0:T(4,128)(2,1)S(1)} %get-tuple-element.2195), channel_id=1, source_target_pairs={{0,7},{1,6},{2,5},{3,4},{4,3},{5,2},{6,1},{7,0},{8,15},{9,14},{10,... | collective-permute-start | bytes 393224 | tf_op jit(solution)/shard_map/ppermute | solution.py:197
  1042.7 16.9 %collective-permute-start.8 = (bf16[2,64,4,128]{3,2,1,0:T(4,128)(2,1)S(1)}, bf16[2,64,4,128]{3,2,1,0:T(4,128)(2,1)S(1)}, u32[]{:S(2)}, u32[]{:S(2)}) collective-permute-start(bf16[2,64,4,128]{3,2,1,0:T(4,128)(2,1)S(1)} %get-tuple-element.2194), channel_id=1, source_target_pairs={{0,8},{1,9},{2,10},{3,11},{4,12},{5,13},{6,14},{7,15},{8,0},{9,1},... | collective-permute-start | bytes 393224 | tf_op jit(solution)/shard_map/ppermute | solution.py:197
  1042.9 21.9 %collective-permute-start.9 = (bf16[2,64,4,128]{3,2,1,0:T(4,128)(2,1)S(1)}, bf16[2,64,4,128]{3,2,1,0:T(4,128)(2,1)S(1)}, u32[]{:S(2)}, u32[]{:S(2)}) collective-permute-start(bf16[2,64,4,128]{3,2,1,0:T(4,128)(2,1)S(1)} %get-tuple-element.2193), channel_id=1, source_target_pairs={{0,9},{1,8},{2,11},{3,10},{4,13},{5,12},{6,15},{7,14},{8,1},{9,0},... | collective-permute-start | bytes 393224 | tf_op jit(solution)/shard_map/ppermute | solution.py:197
  1046.5 22.7 %collective-permute-start.10 = (bf16[2,64,4,128]{3,2,1,0:T(4,128)(2,1)S(1)}, bf16[2,64,4,128]{3,2,1,0:T(4,128)(2,1)S(1)}, u32[]{:S(2)}, u32[]{:S(2)}) collective-permute-start(bf16[2,64,4,128]{3,2,1,0:T(4,128)(2,1)S(1)} %get-tuple-element.2192), channel_id=1, source_target_pairs={{0,10},{1,11},{2,8},{3,9},{4,14},{5,15},{6,12},{7,13},{8,2},{9,3},... | collective-permute-start | bytes 393224 | tf_op jit(solution)/shard_map/ppermute | solution.py:197
  1049.7 23.9 %collective-permute-start.11 = (bf16[2,64,4,128]{3,2,1,0:T(4,128)(2,1)S(1)}, bf16[2,64,4,128]{3,2,1,0:T(4,128)(2,1)S(1)}, u32[]{:S(2)}, u32[]{:S(2)}) collective-permute-start(bf16[2,64,4,128]{3,2,1,0:T(4,128)(2,1)S(1)} %get-tuple-element.2191), channel_id=1, source_target_pairs={{0,11},{1,10},{2,9},{3,8},{4,15},{5,14},{6,13},{7,12},{8,3},{9,2},... | collective-permute-start | bytes 393224 | tf_op jit(solution)/shard_map/ppermute | solution.py:197
  1052.0 21.7 %collective-permute-start.12 = (bf16[2,64,4,128]{3,2,1,0:T(4,128)(2,1)S(1)}, bf16[2,64,4,128]{3,2,1,0:T(4,128)(2,1)S(1)}, u32[]{:S(2)}, u32[]{:S(2)}) collective-permute-start(bf16[2,64,4,128]{3,2,1,0:T(4,128)(2,1)S(1)} %get-tuple-element.2190), channel_id=1, source_target_pairs={{0,12},{1,13},{2,14},{3,15},{4,8},{5,9},{6,10},{7,11},{8,4},{9,5},... | collective-permute-start | bytes 393224 | tf_op jit(solution)/shard_map/ppermute | solution.py:197
  1059.6 14.3 %collective-permute-start.13 = (bf16[2,64,4,128]{3,2,1,0:T(4,128)(2,1)S(1)}, bf16[2,64,4,128]{3,2,1,0:T(4,128)(2,1)S(1)}, u32[]{:S(2)}, u32[]{:S(2)}) collective-permute-start(bf16[2,64,4,128]{3,2,1,0:T(4,128)(2,1)S(1)} %get-tuple-element.2189), channel_id=1, source_target_pairs={{0,13},{1,12},{2,15},{3,14},{4,9},{5,8},{6,11},{7,10},{8,5},{9,4},... | collective-permute-start | bytes 393224 | tf_op jit(solution)/shard_map/ppermute | solution.py:197
  1064.8 9.1 collective-permute-start.14
  1069.2 8.7 collective-permute-start.15
  (33 other events, 96.7 us)
